TPU v7x, 256 devices: a whole 4x4x8 slice. The times are simulated.
256 devices in a mesh: dp: 16 (over x_hi, z), param: 16 (over y, x_lo, core).
Axes of the slice: x: 4 (x_hi: 2, x_lo: 2; x = x_hi * 2 + x_lo), y: 4, z: 8, core: 2. Of those that a mesh axis runs over, the one named last changes fastest.
Arguments:
- ex_grads: bfloat16 [1536, 20480], P('dp', 'param'), may hold values from -6 to 6
- tgt_grads: bfloat16 [4096, 20480], P('dp', 'param'), may hold values from -6 to 6
- projection: bfloat16 [20480, 4096], P('param'), may hold values from -0.0390625 to 0.0390625
- example_weight: float32 [1536], P('param'), may hold values from 0.05 to 1
Outputs:
- scores: float32 [4096, 1536], P('dp', 'param')
All inputs are finite; a program needn't handle non-finite values.
Results may differ from a plain program's by a relative error of at most 0.0078.
Values may be sent and summed in bfloat16 or wider, within the bound.
A program may use at most 192 MiB of HBM per device.

v0:
```python
import math
import jax
import jax.numpy as jnp
from jax import lax
from jax.sharding import PartitionSpec as P

ridge_value = 0.5


def sent_to_all(x, axis):
    length = lax.axis_size(axis)
    return lax.all_to_all(jnp.broadcast_to(x[None], (length, *x.shape)), axis, 0, 0, tiled=True)


def in_order(parts, dim):
    parts = jnp.moveaxis(parts, 0, dim)
    lengths = parts.shape
    return parts.reshape(*lengths[:dim], lengths[dim] * lengths[dim + 1], *lengths[dim + 2 :])


def gather_directly(x, axis, dim):
    parts = sent_to_all(x, axis)
    return in_order(parts, dim)


def with_ridge(block, first_row):
    row_ids = lax.broadcasted_iota(jnp.int32, block.shape, 0) + first_row
    col_ids = lax.broadcasted_iota(jnp.int32, block.shape, 1)
    return block + jnp.where(row_ids == col_ids, ridge_value, 0.0).astype(jnp.float32)


def on_device(ex_grads, tgt_grads, projection, example_weight):
    ex_rows = ex_grads.shape[0]
    columns = projection.shape[1]
    param_total = lax.axis_size("param")
    param_pos = lax.axis_index("param")
    replica_pos = lax.axis_index("dp")
    stacked = jnp.concatenate([ex_grads, tgt_grads], axis=0)
    contract_rows = (((0,), (1,)), ((), ()))
    feature_block = lax.psum_scatter(
        lax.dot_general(projection, stacked, contract_rows, preferred_element_type=jnp.float32),
        "param",
        scatter_dimension=0,
        tiled=True,
    )
    local_features = feature_block.astype(jnp.bfloat16)
    example_part = local_features[:, :ex_rows]
    contract_first = (((0,), (0,)), ((), ()))
    partial_value = lax.dot_general(
        local_features,
        gather_directly(example_part, "dp", 1),
        contract_first,
        preferred_element_type=jnp.float32,
    )
    examples = partial_value.shape[1]
    summed = lax.psum(partial_value, "param")
    kernel_block = with_ridge(summed[:ex_rows] / columns, replica_pos * ex_rows)
    kernel = lax.all_gather(kernel_block, "dp", axis=0, tiled=True)
    cross_terms = summed[ex_rows:] / columns
    factor = jnp.linalg.cholesky(kernel)
    forward = jax.scipy.linalg.solve_triangular(factor, cross_terms.T, lower=True)
    solved = jax.scipy.linalg.solve_triangular(factor, forward, lower=True, trans=1)
    block_cols = examples // param_total
    chosen = lax.dynamic_slice_in_dim(solved.T, param_pos * block_cols, block_cols, 1)
    return chosen * math.sqrt(columns) * example_weight[None, :]


def solution(mesh):
    placed = (P("dp", "param"), P("dp", "param"), P("param", None), P("param"))
    return jax.shard_map(
        on_device, mesh=mesh, in_specs=placed, out_specs=P("dp", "param"), check_vma=False
    )
```

profile of v0, /device:TPU:1, one launch (start us, length us, event | category | flops | bytes accessed | tf_op | source)
XLA Modules:
  0.0 965.1 jit_solution(2935307158991540555)
XLA Ops:
  6.5 10.7 %convolution_bitcast_fusion = f32[4096,352]{0,1:T(8,128)} fusion(bf16[1280,4096]{1,0:T(8,128)(2,1)} %param.6, bf16[256,1280]{1,0:T(8,128)(2,1)} %param.5, bf16[96,1280]{1,0:T(8,128)(2,1)} %param.4), kind=kOutput, calls=%fused_computation.6 | convolution fusion | flops 3692789760 | bytes 17154048 | tf_op jit(solution)/shard_map/dot_general | solution.py:41
  17.3 79.7 %reduce-scatter.2.cloned.1.call-done = f32[256,352]{0,1:T(8,128)} async-done(((f32[4096,352]{0,1:T(8,128)}), f32[256,352]{0,1:T(8,128)}) %reduce-scatter.2.cloned.1.call-update) | async-done | bytes 360464 | tf_op jit(solution)/shard_map/reduce_scatter | solution.py:40
  98.1 27.1 %all_to_all.5 = bf16[16,256,96]{1,2,0:T(8,128)(2,1)S(1)} all-to-all(bf16[16,256,96]{1,2,0:T(8,128)(2,1)S(1)} %broadcast_in_dim.17), channel_id=1, replica_groups=mesh['dp'=16,'param'=16] {'dp'}, dimensions={0} | all-to-all | bytes 1572864 | tf_op jit(solution)/shard_map/all_to_all | solution.py:12
  127.1 130.4 %all-reduce.3.cloned.1.call-done = f32[352,1536]{1,0:T(8,128)} async-done(((f32[352,1536]{1,0:T(8,128)}), f32[352,1536]{1,0:T(8,128)}) %all-reduce.3.cloned.1.call-update) | async-done | bytes 2162704 | tf_op jit(solution)/shard_map/psum | solution.py:56
  261.1 144.9 %all-gather.2.cloned.1.call-done = f32[1536,1536]{1,0:T(8,128)} async-done(((f32[96,1536]{1,0:T(8,128)}), f32[1536,1536]{1,0:T(8,128)}) %all-gather.2.cloned.1.call-update) | async-done | bytes 9437200 | tf_op jit(solution)/shard_map/all_gather | solution.py:58
  406.0 10.1 %copy.10 = f32[1536,1536]{0,1:T(8,128)} copy(f32[1536,1536]{1,0:T(8,128)} %all-gather.2.cloned.1.call-done) | data formatting | bytes 18874368 | tf_op jit(solution)/shard_map/all_gather | solution.py:58
  416.1 12.3 %fusion = f32[1536,1536]{1,0:T(8,128)} fusion(f32[1536,1536]{1,0:T(8,128)} %all-gather.2.cloned.1.call-done, f32[1536,1536]{0,1:T(8,128)} %copy.10), kind=kLoop, calls=%fused_computation.4 | loop fusion | flops 4718592 | bytes 28311552 | tf_op jit(solution)/shard_map/jit(cholesky)/div | solution.py:60
  429.3 11.7 %cholesky.341 = f32[128,128]{1,0:T(8,128)S(1)} custom-call(f32[128,128]{1,0:T(8,128)S(1)} %cholesky.892), custom_call_target="Cholesky" | custom-call | tf_op jit(solution)/shard_map/jit(cholesky)/cholesky | solution.py:60
  445.8 9.8 %custom-call.98 = f32[1,128,128]{1,2,0:T(8,128)S(1)} custom-call(f32[1,128,128]{2,1,0:T(8,128)S(1)} %get-tuple-element.111), custom_call_target="InvertDiagBlocksLowerTriangular" | custom-call | tf_op jit(solution)/shard_map/jit(cholesky)/cholesky | solution.py:60
  460.3 11.9 %cholesky.362 = f32[128,128]{1,0:T(8,128)S(1)} custom-call(f32[128,128]{1,0:T(8,128)S(1)} %cholesky.896), custom_call_target="Cholesky" | custom-call | tf_op jit(solution)/shard_map/jit(cholesky)/cholesky | solution.py:60
  472.9 9.8 %custom-call.99 = f32[1,128,128]{1,2,0:T(8,128)S(1)} custom-call(f32[1,128,128]{2,1,0:T(8,128)S(1)} %get-tuple-element.108), custom_call_target="InvertDiagBlocksLowerTriangular" | custom-call | tf_op jit(solution)/shard_map/jit(cholesky)/cholesky | solution.py:60
  487.0 11.7 %cholesky.385 = f32[128,128]{1,0:T(8,128)S(1)} custom-call(f32[128,128]{1,0:T(8,128)S(1)} %cholesky.901), custom_call_target="Cholesky" | custom-call | tf_op jit(solution)/shard_map/jit(cholesky)/cholesky | solution.py:60
  499.4 10.0 %custom-call.100 = f32[1,128,128]{1,2,0:T(8,128)S(1)} custom-call(f32[1,128,128]{2,1,0:T(8,128)S(1)} %get-tuple-element.105), custom_call_target="InvertDiagBlocksLowerTriangular" | custom-call | tf_op jit(solution)/shard_map/jit(cholesky)/cholesky | solution.py:60
  514.3 11.7 %cholesky.715 = f32[128,128]{1,0:T(8,128)S(1)} custom-call(f32[128,128]{1,0:T(8,128)S(1)} %cholesky.906), custom_call_target="Cholesky" | custom-call | tf_op jit(solution)/shard_map/jit(cholesky)/cholesky | solution.py:60
  526.6 9.8 %custom-call.101 = f32[1,128,128]{1,2,0:T(8,128)S(1)} custom-call(f32[1,128,128]{2,1,0:T(8,128)S(1)} %get-tuple-element.102), custom_call_target="InvertDiagBlocksLowerTriangular" | custom-call | tf_op jit(solution)/shard_map/jit(cholesky)/cholesky | solution.py:60
  541.4 12.1 %cholesky.734 = f32[128,128]{1,0:T(8,128)S(1)} custom-call(f32[128,128]{1,0:T(8,128)S(1)} %cholesky.911), custom_call_target="Cholesky" | custom-call | tf_op jit(solution)/shard_map/jit(cholesky)/cholesky | solution.py:60
  554.2 9.8 %custom-call.102 = f32[1,128,128]{1,2,0:T(8,128)S(1)} custom-call(f32[1,128,128]{2,1,0:T(8,128)S(1)} %get-tuple-element.99), custom_call_target="InvertDiagBlocksLowerTriangular" | custom-call | tf_op jit(solution)/shard_map/jit(cholesky)/cholesky | solution.py:60
  569.1 11.7 %cholesky.754 = f32[128,128]{1,0:T(8,128)S(1)} custom-call(f32[128,128]{1,0:T(8,128)S(1)} %cholesky.916), custom_call_target="Cholesky" | custom-call | tf_op jit(solution)/shard_map/jit(cholesky)/cholesky | solution.py:60
  581.5 10.0 %custom-call.103 = f32[1,128,128]{1,2,0:T(8,128)S(1)} custom-call(f32[1,128,128]{2,1,0:T(8,128)S(1)} %get-tuple-element.96), custom_call_target="InvertDiagBlocksLowerTriangular" | custom-call | tf_op jit(solution)/shard_map/jit(cholesky)/cholesky | solution.py:60
  596.6 11.7 %cholesky.774 = f32[128,128]{1,0:T(8,128)S(1)} custom-call(f32[128,128]{1,0:T(8,128)S(1)} %cholesky.921), custom_call_target="Cholesky" | custom-call | tf_op jit(solution)/shard_map/jit(cholesky)/cholesky | solution.py:60
  609.0 9.8 %custom-call.104 = f32[1,128,128]{1,2,0:T(8,128)S(1)} custom-call(f32[1,128,128]{2,1,0:T(8,128)S(1)} %get-tuple-element.93), custom_call_target="InvertDiagBlocksLowerTriangular" | custom-call | tf_op jit(solution)/shard_map/jit(cholesky)/cholesky | solution.py:60
  624.1 11.7 %cholesky.794 = f32[128,128]{1,0:T(8,128)S(1)} custom-call(f32[128,128]{1,0:T(8,128)S(1)} %cholesky.926), custom_call_target="Cholesky" | custom-call | tf_op jit(solution)/shard_map/jit(cholesky)/cholesky | solution.py:60
  636.5 9.8 %custom-call.105 = f32[1,128,128]{1,2,0:T(8,128)S(1)} custom-call(f32[1,128,128]{2,1,0:T(8,128)S(1)} %get-tuple-element.90), custom_call_target="InvertDiagBlocksLowerTriangular" | custom-call | tf_op jit(solution)/shard_map/jit(cholesky)/cholesky | solution.py:60
  650.9 12.2 %cholesky.814 = f32[128,128]{1,0:T(8,128)S(1)} custom-call(f32[128,128]{1,0:T(8,128)S(1)} %cholesky.931), custom_call_target="Cholesky" | custom-call | tf_op jit(solution)/shard_map/jit(cholesky)/cholesky | solution.py:60
  663.7 9.8 %custom-call.106 = f32[1,128,128]{1,2,0:T(8,128)S(1)} custom-call(f32[1,128,128]{2,1,0:T(8,128)S(1)} %get-tuple-element.87), custom_call_target="InvertDiagBlocksLowerTriangular" | custom-call | tf_op jit(solution)/shard_map/jit(cholesky)/cholesky | solution.py:60
  677.9 11.7 %cholesky.834 = f32[128,128]{1,0:T(8,128)S(1)} custom-call(f32[128,128]{1,0:T(8,128)S(1)} %cholesky.936), custom_call_target="Cholesky" | custom-call | tf_op jit(solution)/shard_map/jit(cholesky)/cholesky | solution.py:60
  690.2 9.8 %custom-call.107 = f32[1,128,128]{1,2,0:T(8,128)S(1)} custom-call(f32[1,128,128]{2,1,0:T(8,128)S(1)} %get-tuple-element.84), custom_call_target="InvertDiagBlocksLowerTriangular" | custom-call | tf_op jit(solution)/shard_map/jit(cholesky)/cholesky | solution.py:60
  703.7 11.9 %cholesky.854 = f32[128,128]{1,0:T(8,128)S(1)} custom-call(f32[128,128]{1,0:T(8,128)S(1)} %cholesky.941), custom_call_target="Cholesky" | custom-call | tf_op jit(solution)/shard_map/jit(cholesky)/cholesky | solution.py:60
  716.2 9.8 %custom-call.108 = f32[1,128,128]{1,2,0:T(8,128)S(1)} custom-call(f32[1,128,128]{2,1,0:T(8,128)S(1)} %get-tuple-element.81), custom_call_target="InvertDiagBlocksLowerTriangular" | custom-call | tf_op jit(solution)/shard_map/jit(cholesky)/cholesky | solution.py:60
  729.2 11.7 %cholesky.872 = f32[128,128]{1,0:T(8,128)S(1)} custom-call(f32[128,128]{1,0:T(8,128)S(1)} %convolution_subtract_fusion.25), custom_call_target="Cholesky" | custom-call | tf_op jit(solution)/shard_map/jit(cholesky)/cholesky | solution.py:60
  765.2 35.2 %while.1 = (s32[]{:T(128)}, f32[1536,1536]{1,0:T(8,128)}, s32[12,2]{0,1:T(2,128)S(1)}, f32[12,128,128]{2,1,0:T(8,128)S(1)}, s32[]{:T(128)}) while((s32[]{:T(128)}, f32[1536,1536]{1,0:T(8,128)}, s32[12,2]{0,1:T(2,128)S(1)}, f32[12,128,128]{2,1,0:T(8,128)S(1)}, s32[]{:T(128)}) %tuple.106), condition=%wide.while_cond, body=%wide.while_body.sunk | while | flops 2 | bytes 131189 | solution.py:62
  800.4 118.3 %custom-call.109 = f32[12,128,128]{1,2,0:T(8,128)S(1)} custom-call(f32[12,128,128]{2,1,0:T(8,128)S(1)} %get-tuple-element.12), custom_call_target="InvertDiagBlocksLowerTriangular" | custom-call | tf_op jit(solution)/shard_map/jit(_solve_triangular)/triangular_solve | solution.py:62
  (222 shorter events, 159.5 us)
Async XLA Ops:
  6.5 90.4 %reduce-scatter.2.cloned.1.call-start = ((), (), s32[]{:S(2)}) async-start(), calls=%async_computation.2 | async-start | bytes 6127616 | tf_op jit(solution)/shard_map/reduce_scatter | solution.py:40
  17.2 240.3 %all-reduce.3.cloned.1.call-start = ((), (), s32[]{:S(2)}) async-start(), calls=%async_computation.3 | async-start | bytes 4325376 | tf_op jit(solution)/shard_map/psum | solution.py:56
  127.0 132.5 %copy-start.1 = (f32[96]{0:T(128)S(1)}, f32[96]{0:T(128)}, u32[]{:S(2)}) copy-start(f32[96]{0:T(128)} %param.7) | copy-start | bytes 1156
  127.1 278.9 %all-gather.2.cloned.1.call-start = ((), (), s32[]{:S(2)}) async-start(), calls=%async_computation.4 | async-start | bytes 10027008 | tf_op jit(solution)/shard_map/all_gather | solution.py:58
  920.3 9.7 %copy-start = (f32[1536,1536]{1,0:T(8,128)S(1)}, f32[1536,1536]{1,0:T(8,128)}, u32[]{:S(2)}) copy-start(f32[1536,1536]{1,0:T(8,128)} %get-tuple-element.190) | copy-start | bytes 28311556
Sparse Core Ops, SparseCore 0:
  17.4 79.5 reduce-scatter.1
  127.2 130.2 all-reduce.2
  260.1 145.8 all-gather.1
where the time goes:
time: 970 us; the launch traced here: 965 us
  other arithmetic  409 us (42%)
  waiting for transfers between devices  355 us (37%)
  matrix products  100 us (10%)
  local copies, waits for them, and re-layouts  51.6 us (5%)
  blocking collectives  27.1 us (3%)
  between operations  22.1 us (2%)
    another operation x46, other arithmetic, on_device(): factor = jnp.linalg.cholesky(kernel)  265 us
    all_gather x1, waiting for transfers between devices, on_device(): kernel = lax.all_gather(kernel_block, 'dp', axis=0, tiled=True)  145 us
    psum x1, waiting for transfers between devices, on_device(): summed = lax.psum(partial_value, 'param')  130 us
    another operation x3, other arithmetic, on_device(): jax.scipy.linalg.solve_triangular(factor, forward, lower=True, trans=1)  127 us
    reduce_scatter x1, waiting for transfers between devices, on_device(): lax.psum_scatter(lax.dot_general(projection, stacked, contract_rows, pref...  79.7 us
    another operation x22, matrix products, on_device(): factor = jnp.linalg.cholesky(kernel)  50.1 us
    another operation x36, local copies, waits for them, and re-layouts  35 us
    all_to_all x1, blocking collectives, sent_to_all(): lax.all_to_all(jnp.broadcast_to(x[None], (length, *x.shape)), axis, 0, 0,...  27.1 us
  transfers between devices with their start and end apart: 3, of which 3 were waited for; matrix products, arithmetic and copies ran while one was open for 0% of the time, Pallas kernels for 0%

commit v1 on v0

--- a/solution.py
+++ b/solution.py
@@ -55,7 +55,10 @@
     examples = partial_value.shape[1]
     summed = lax.psum(partial_value, "param")
     kernel_block = with_ridge(summed[:ex_rows] / columns, replica_pos * ex_rows)
-    kernel = lax.all_gather(kernel_block, "dp", axis=0, tiled=True)
+    frame_out = lax.all_to_all(
+        jnp.stack(lax.axis_size("dp") * [kernel_block]), axis_name="dp", split_axis=0, concat_axis=0
+    )
+    kernel = jnp.concatenate(frame_out, axis=0)
     cross_terms = summed[ex_rows:] / columns
     factor = jnp.linalg.cholesky(kernel)
     forward = jax.scipy.linalg.solve_triangular(factor, cross_terms.T, lower=True)

time: 970 us -> 1060 us (1.093); the launches traced: 965 us -> 1040 us
  waiting for transfers between devices: 355 us -> 417 us
    all_to_all x0 -> x1, waiting for transfers between devices: none -> 207 us  [on_device(): lax.all_to_all(jnp.stack(lax.axis_size('dp') * [kernel_block]), axis_name...]
    all_gather x1 -> x0, waiting for transfers between devices: 145 us -> none  [on_device(): kernel = lax.all_gather(kernel_block, 'dp', axis=0, tiled=True)]
    another operation x36 -> x37, local copies, waits for them, and re-layouts: 35 us -> 39.7 us
where the time goes in v1:
time: 1060 us; the launch traced here: 1040 us
  waiting for transfers between devices  417 us (39%)
  other arithmetic  408 us (38%)
  matrix products  100 us (9%)
  local copies, waits for them, and re-layouts  56.4 us (5%)
  blocking collectives  27.1 us (3%)
  between operations  22.4 us (2%)
    another operation x46, other arithmetic, on_device(): factor = jnp.linalg.cholesky(kernel)  265 us
    all_to_all x1, waiting for transfers between devices, on_device(): lax.all_to_all(jnp.stack(lax.axis_size('dp') * [kernel_block]), axis_name...  207 us
    psum x1, waiting for transfers between devices, on_device(): summed = lax.psum(partial_value, 'param')  130 us
    another operation x3, other arithmetic, on_device(): jax.scipy.linalg.solve_triangular(factor, forward, lower=True, trans=1)  127 us
    reduce_scatter x1, waiting for transfers between devices, on_device(): lax.psum_scatter(lax.dot_general(projection, stacked, contract_rows, pref...  79.7 us
    another operation x22, matrix products, on_device(): factor = jnp.linalg.cholesky(kernel)  50.1 us
    another operation x36, local copies, waits for them, and re-layouts  35 us
    all_to_all x1, blocking collectives, sent_to_all(): lax.all_to_all(jnp.broadcast_to(x[None], (length, *x.shape)), axis, 0, 0,...  27.1 us
  transfers between devices with their start and end apart: 3, of which 3 were waited for; matrix products, arithmetic and copies ran while one was open for 0% of the time, Pallas kernels for 0%

profile of v1, /device:TPU:1, one launch (start us, length us, event | category | flops | bytes accessed | tf_op | source)
XLA Modules:
  0.0 1040.4 jit_solution(2385448750648486340)
XLA Ops:
  6.5 10.7 %convolution_bitcast_fusion = f32[4096,352]{0,1:T(8,128)} fusion(bf16[1280,4096]{1,0:T(8,128)(2,1)} %param.6, bf16[256,1280]{1,0:T(8,128)(2,1)} %param.5, bf16[96,1280]{1,0:T(8,128)(2,1)} %param.4), kind=kOutput, calls=%fused_computation.6 | convolution fusion | flops 3692789760 | bytes 17154048 | tf_op jit(solution)/shard_map/dot_general | solution.py:41
  17.3 79.7 %reduce-scatter.2.cloned.1.call-done = f32[256,352]{0,1:T(8,128)} async-done(((f32[4096,352]{0,1:T(8,128)}), f32[256,352]{0,1:T(8,128)}) %reduce-scatter.2.cloned.1.call-update) | async-done | bytes 360464 | tf_op jit(solution)/shard_map/reduce_scatter | solution.py:40
  98.1 27.1 %all_to_all.10 = bf16[16,256,96]{1,2,0:T(8,128)(2,1)S(1)} all-to-all(bf16[16,256,96]{1,2,0:T(8,128)(2,1)S(1)} %broadcast_in_dim.17), channel_id=1, replica_groups=mesh['dp'=16,'param'=16] {'dp'}, dimensions={0} | all-to-all | bytes 1572864 | tf_op jit(solution)/shard_map/all_to_all | solution.py:12
  127.1 130.4 %all-reduce.3.cloned.1.call-done = f32[352,1536]{1,0:T(8,128)} async-done(((f32[352,1536]{1,0:T(8,128)}), f32[352,1536]{1,0:T(8,128)}) %all-reduce.3.cloned.1.call-update) | async-done | bytes 2162704 | tf_op jit(solution)/shard_map/psum | solution.py:56
  274.0 207.0 %all-to-all-done.1 = f32[16,96,1536]{2,1,0:T(8,128)} async-done(((f32[16,96,1536]{2,1,0:T(8,128)}), f32[16,96,1536]{2,1,0:T(8,128)}, u32[]{:S(2)}, u32[]{:S(2)}) %all-to-all-start.1) | async-done | bytes 9437216 | tf_op jit(solution)/shard_map/all_to_all | solution.py:58
  481.0 10.1 copy.8
  491.1 12.3 %fusion = f32[1536,1536]{1,0:T(8,128)} fusion(f32[1536,1536]{0,1:T(8,128)} %copy.8, f32[16,96,1536]{2,1,0:T(8,128)} %all-to-all-done.1), kind=kLoop, calls=%fused_computation.4 | loop fusion | flops 4718592 | bytes 28311552 | tf_op jit(solution)/shard_map/jit(cholesky)/div | solution.py:63
  504.2 11.7 %cholesky.341 = f32[128,128]{1,0:T(8,128)S(1)} custom-call(f32[128,128]{1,0:T(8,128)S(1)} %cholesky.892), custom_call_target="Cholesky" | custom-call | tf_op jit(solution)/shard_map/jit(cholesky)/cholesky | solution.py:63
  520.8 9.8 custom-call.98
  535.3 11.9 %cholesky.362 = f32[128,128]{1,0:T(8,128)S(1)} custom-call(f32[128,128]{1,0:T(8,128)S(1)} %cholesky.896), custom_call_target="Cholesky" | custom-call | tf_op jit(solution)/shard_map/jit(cholesky)/cholesky | solution.py:63
  547.8 9.8 custom-call.99
  562.0 11.7 %cholesky.385 = f32[128,128]{1,0:T(8,128)S(1)} custom-call(f32[128,128]{1,0:T(8,128)S(1)} %cholesky.901), custom_call_target="Cholesky" | custom-call | tf_op jit(solution)/shard_map/jit(cholesky)/cholesky | solution.py:63
  574.4 10.0 custom-call.100
  589.2 11.7 %cholesky.715 = f32[128,128]{1,0:T(8,128)S(1)} custom-call(f32[128,128]{1,0:T(8,128)S(1)} %cholesky.906), custom_call_target="Cholesky" | custom-call | tf_op jit(solution)/shard_map/jit(cholesky)/cholesky | solution.py:63
  601.6 9.8 custom-call.101
  616.4 12.1 %cholesky.734 = f32[128,128]{1,0:T(8,128)S(1)} custom-call(f32[128,128]{1,0:T(8,128)S(1)} %cholesky.911), custom_call_target="Cholesky" | custom-call | tf_op jit(solution)/shard_map/jit(cholesky)/cholesky | solution.py:63
  629.2 9.8 custom-call.102
  644.1 11.7 %cholesky.754 = f32[128,128]{1,0:T(8,128)S(1)} custom-call(f32[128,128]{1,0:T(8,128)S(1)} %cholesky.916), custom_call_target="Cholesky" | custom-call | tf_op jit(solution)/shard_map/jit(cholesky)/cholesky | solution.py:63
  656.5 10.0 custom-call.103
  671.6 11.7 %cholesky.774 = f32[128,128]{1,0:T(8,128)S(1)} custom-call(f32[128,128]{1,0:T(8,128)S(1)} %cholesky.921), custom_call_target="Cholesky" | custom-call | tf_op jit(solution)/shard_map/jit(cholesky)/cholesky | solution.py:63
  684.0 9.8 custom-call.104
  699.1 11.7 %cholesky.794 = f32[128,128]{1,0:T(8,128)S(1)} custom-call(f32[128,128]{1,0:T(8,128)S(1)} %cholesky.926), custom_call_target="Cholesky" | custom-call | tf_op jit(solution)/shard_map/jit(cholesky)/cholesky | solution.py:63
  711.4 9.8 custom-call.105
  725.9 12.2 %cholesky.814 = f32[128,128]{1,0:T(8,128)S(1)} custom-call(f32[128,128]{1,0:T(8,128)S(1)} %cholesky.931), custom_call_target="Cholesky" | custom-call | tf_op jit(solution)/shard_map/jit(cholesky)/cholesky | solution.py:63
  738.7 9.8 custom-call.106
  752.9 11.7 %cholesky.834 = f32[128,128]{1,0:T(8,128)S(1)} custom-call(f32[128,128]{1,0:T(8,128)S(1)} %cholesky.936), custom_call_target="Cholesky" | custom-call | tf_op jit(solution)/shard_map/jit(cholesky)/cholesky | solution.py:63
  765.2 9.8 custom-call.107
  778.7 11.9 %cholesky.854 = f32[128,128]{1,0:T(8,128)S(1)} custom-call(f32[128,128]{1,0:T(8,128)S(1)} %cholesky.941), custom_call_target="Cholesky" | custom-call | tf_op jit(solution)/shard_map/jit(cholesky)/cholesky | solution.py:63
  791.2 9.8 custom-call.108
  804.2 11.7 %cholesky.872 = f32[128,128]{1,0:T(8,128)S(1)} custom-call(f32[128,128]{1,0:T(8,128)S(1)} %convolution_subtract_fusion.25), custom_call_target="Cholesky" | custom-call | tf_op jit(solution)/shard_map/jit(cholesky)/cholesky | solution.py:63
  840.2 35.2 %while.1 = (s32[]{:T(128)}, f32[1536,1536]{1,0:T(8,128)}, s32[12,2]{0,1:T(2,128)S(1)}, f32[12,128,128]{2,1,0:T(8,128)S(1)}, s32[]{:T(128)}) while((s32[]{:T(128)}, f32[1536,1536]{1,0:T(8,128)}, s32[12,2]{0,1:T(2,128)S(1)}, f32[12,128,128]{2,1,0:T(8,128)S(1)}, s32[]{:T(128)}) %tuple.106), condition=%wide.while_cond, body=%wide.while_body.sunk | while | flops 2 | bytes 131189 | solution.py:65
  875.4 118.3 %custom-call.109 = f32[12,128,128]{1,2,0:T(8,128)S(1)} custom-call(f32[12,128,128]{2,1,0:T(8,128)S(1)} %get-tuple-element.12), custom_call_target="InvertDiagBlocksLowerTriangular" | custom-call | tf_op jit(solution)/shard_map/jit(_solve_triangular)/triangular_solve | solution.py:65
  (222 shorter events, 172.3 us)
Async XLA Ops:
  6.5 90.4 %reduce-scatter.2.cloned.1.call-start = ((), (), s32[]{:S(2)}) async-start(), calls=%async_computation.3 | async-start | bytes 6127616 | tf_op jit(solution)/shard_map/reduce_scatter | solution.py:40
  17.2 240.3 %all-reduce.3.cloned.1.call-start = ((), (), s32[]{:S(2)}) async-start(), calls=%async_computation.4 | async-start | bytes 4325376 | tf_op jit(solution)/shard_map/psum | solution.py:56
  263.4 9.0 copy-start.1
  263.5 217.6 %all-to-all-start.1 = ((f32[16,96,1536]{2,1,0:T(8,128)}), f32[16,96,1536]{2,1,0:T(8,128)}, u32[]{:S(2)}, u32[]{:S(2)}) async-start(f32[16,96,1536]{2,1,0:T(8,128)} %stack.2), calls=%async_computation.2 | async-start | bytes 18874368 | tf_op jit(solution)/shard_map/all_to_all | solution.py:58
  995.3 9.7 copy-start
Sparse Core Ops, SparseCore 0:
  17.4 79.5 reduce-scatter.1
  127.2 130.2 all-reduce.2
